TPU v7x, 32 devices: a whole 2x2x4 slice. The times are simulated.
32 devices in a mesh: pop: 8 (over z, x), mp: 4 (over y, core).
Axes of the slice: x: 2, y: 2, z: 4, core: 2. Of those that a mesh axis runs over, the one named last changes fastest.
Arguments:
- tokens: bfloat16 [256, 3584], replicated, may hold values from -60 to 60
- target: bfloat16 [256, 3584], P(None, 'mp'), may hold values from -6 to 6
- w_query: bfloat16 [3584, 3584], P('pop', 'mp'), may hold values from -0.09375 to 0.09375
- w_key: bfloat16 [3584, 512], P(None, 'mp'), may hold values from -0.09375 to 0.09375
- w_value: bfloat16 [3584, 512], P(None, 'mp'), may hold values from -0.09375 to 0.09375
- w_out: bfloat16 [3584, 3584], P('mp', 'pop'), may hold values from -0.09375 to 0.09375
- query_left_factors: bfloat16 [8, 3584, 4], P('pop'), may hold values from -0.09375 to 0.09375
- query_right_factors: bfloat16 [8, 4, 3584], P('pop', None, 'mp'), may hold values from -6 to 6
- o_left: bfloat16 [8, 3584, 4], P('pop', 'mp'), may hold values from -0.09375 to 0.09375
- o_right: bfloat16 [8, 4, 3584], P('pop'), may hold values from -6 to 6
- member_ids: int32 [8], P('pop'), may hold values from 0 to 7, each once
Outputs:
- grad_query: float32 [3584, 3584], P('pop', 'mp')
- grad_out: float32 [3584, 3584], P('mp', 'pop')
- fitness: float32 [8], P('pop')
Inputs may be any that keep to these rules, and one draw needn't show every extreme that they name: `member_ids`: every number from 0 to 7 appears once.
All inputs are finite; a program needn't handle non-finite values.
Results may differ from a plain program's by a relative error of at most 0.005.
Values may be sent and summed in bfloat16 or wider, within the bound.
A program may use at most 64 MiB of HBM per device.

v0:
```python
import math
import jax
import jax.numpy as jnp
from jax import lax
from jax.sharding import PartitionSpec as P

D = 3584
HEADS = 28
KV_HEADS = 4
HEAD_DIM = 128
RANK = 4
noise_scale = 0.5
rope_base = 1000000.0
spread_floor = 0.001


def tables(count, head_size):
    position = jnp.arange(count, dtype=jnp.float32)
    index = jnp.arange(head_size // 2, dtype=jnp.float32)
    freq = jnp.exp(-math.log(rope_base) * 2.0 * index / head_size)
    angle = position[:, None] * freq[None, :]
    return (jnp.cos(angle)[:, None, :], jnp.sin(angle)[:, None, :])


def rotate(field, cosine_table, sine):
    half = field.shape[-1] // 2
    first = field[..., :half]
    second = field[..., half:]
    return jnp.concatenate(
        [first * cosine_table - second * sine, second * cosine_table + first * sine], axis=-1
    )


def per_device(
    tokens,
    target,
    w_query,
    w_key,
    w_value,
    w_out,
    query_left_factors,
    query_right_factors,
    o_left,
    o_right,
    member_ids,
):
    tok = tokens.shape[0]
    local_feats = w_query.shape[1]
    local_kv = w_key.shape[1] // HEAD_DIM
    group = HEADS // KV_HEADS
    local_heads = local_kv * group
    slots = query_left_factors.shape[0]
    scale = HEAD_DIM ** (-0.5)
    cosine_table, sine = tables(tok, HEAD_DIM)
    base = jnp.dot(
        tokens,
        lax.all_gather(w_query, "pop", axis=0, tiled=True),
        preferred_element_type=jnp.float32,
    )
    keys = rotate(
        jnp.dot(tokens, w_key, preferred_element_type=jnp.float32).reshape(tok, local_kv, HEAD_DIM),
        cosine_table,
        sine,
    ).astype(jnp.bfloat16)
    values = (
        jnp.dot(tokens, w_value, preferred_element_type=jnp.float32)
        .astype(jnp.bfloat16)
        .reshape(tok, local_kv, HEAD_DIM)
    )
    signs = (1 - 2 * (member_ids % 2)).astype(jnp.float32)
    factor = noise_scale * signs[:, None, None]
    lowrank_product = jnp.einsum(
        "td,mdr->mtr", tokens, query_left_factors, preferred_element_type=jnp.float32
    ).astype(jnp.bfloat16)
    query = base[None] + factor * jnp.einsum(
        "olj,ojv->olv", lowrank_product, query_right_factors, preferred_element_type=jnp.float32
    )
    query = rotate(
        query.reshape(slots, tok, local_heads, HEAD_DIM), cosine_table[None], sine[None]
    ).astype(jnp.bfloat16)
    query = query.reshape(slots, tok, local_kv, group, HEAD_DIM)
    scores = jnp.einsum("mtkgd,skd->mkgts", query, keys, preferred_element_type=jnp.float32) * scale
    causal = jnp.arange(tok)[:, None] >= jnp.arange(tok)[None, :]
    scores = jnp.where(causal, scores, -1e30)
    probs = jax.nn.softmax(scores, axis=-1).astype(jnp.bfloat16)
    mixed = (
        jnp.einsum("mkgts,skd->mtkgd", probs, values, preferred_element_type=jnp.float32)
        .astype(jnp.bfloat16)
        .reshape(slots, tok, local_feats)
    )
    low_out = jnp.einsum("mtf,mfr->mtr", mixed, o_left, preferred_element_type=jnp.float32)
    right_full = o_right.astype(jnp.float32)
    part = jnp.einsum(
        "mtf,fe->mte",
        mixed,
        lax.all_gather(w_out, "pop", axis=1, tiled=True),
        preferred_element_type=jnp.float32,
    )
    term = part + factor * jnp.einsum(
        "mtr,mre->mte", low_out, right_full, precision=lax.Precision.HIGHEST
    )
    output = lax.psum_scatter(
        term.astype(jnp.bfloat16), "mp", scatter_dimension=2, tiled=True
    ).astype(jnp.float32)
    diff = output - target.astype(jnp.float32)[None]
    errors = lax.psum(jnp.sum(diff * diff, axis=(1, 2)), "mp")
    fitness = -(errors / (tok * D))
    count = slots * lax.axis_size("pop")
    mean = lax.psum(jnp.sum(fitness), "pop") / count
    spread = lax.psum(jnp.sum((fitness - mean) * (fitness - mean)), "pop") / count
    weight = signs * (fitness - mean) / jnp.sqrt(spread + spread_floor)
    every_weight = lax.all_gather(weight, "pop", axis=0, tiled=True)
    right_factors_gathered, left_all = (
        lax.all_gather(query_right_factors, "pop", axis=0, tiled=True),
        lax.all_gather(o_left, "pop", axis=0, tiled=True),
    )
    rows_q = lax.all_to_all(query_left_factors, "pop", split_axis=1, concat_axis=0, tiled=True)
    cols_o = lax.all_to_all(o_right, "pop", split_axis=2, concat_axis=0, tiled=True)
    whole_population = rows_q.shape[0]
    left_q = jnp.transpose(
        rows_q.astype(jnp.float32) * every_weight[:, None, None], (1, 0, 2)
    ).reshape(rows_q.shape[1], whole_population * RANK)
    right_q = right_factors_gathered.astype(jnp.float32).reshape(
        whole_population * RANK, local_feats
    )
    grad_query = jnp.dot(left_q, right_q, precision=lax.Precision.HIGHEST) / noise_scale
    output_left_factor = jnp.transpose(
        left_all.astype(jnp.float32) * every_weight[:, None, None], (1, 0, 2)
    ).reshape(local_feats, whole_population * RANK)
    right_o = cols_o.astype(jnp.float32).reshape(whole_population * RANK, cols_o.shape[2])
    grad_out = jnp.dot(output_left_factor, right_o, precision=lax.Precision.HIGHEST) / noise_scale
    return (grad_query, grad_out, fitness)


def solution(mesh):
    placed = (
        P(),
        P(None, "mp"),
        P("pop", "mp"),
        P(None, "mp"),
        P(None, "mp"),
        P("mp", "pop"),
        P("pop", None, None),
        P("pop", None, "mp"),
        P("pop", "mp", None),
        P("pop", None, None),
        P("pop"),
    )
    return jax.shard_map(
        per_device,
        mesh=mesh,
        in_specs=placed,
        out_specs=(P("pop", "mp"), P("mp", "pop"), P("pop")),
        check_vma=False,
    )
```

profile of v0, /device:TPU:0, one launch (start us, length us, event | category | flops | bytes accessed | tf_op | source)
XLA Modules:
  0.0 465.0 jit_solution(14919115663158646740)
XLA Ops:
  12.2 101.0 %all-gather.3.cloned.1.call-done = bf16[3584,896]{1,0:T(8,128)(2,1)} async-done(((bf16[448,896]{1,0:T(8,128)(2,1)}), bf16[3584,896]{1,0:T(8,128)(2,1)}) %all-gather.3.cloned.1.call-update) | async-done | bytes 6422544 | tf_op jit(solution)/shard_map/all_gather | solution.py:57
  113.2 4.9 %fusion.37 = f32[256,896]{1,0:T(8,128)S(1)} fusion(bf16[256,3584]{1,0:T(8,128)(2,1)S(1)} %copy-done, bf16[3584,896]{1,0:T(8,128)(2,1)} %all-gather.3.cloned.1.call-done), kind=kOutput, calls=%fused_computation.66 | convolution fusion | flops 1644167168 | bytes 9175040 | tf_op jit(solution)/shard_map/dot_general | solution.py:55
  118.1 2.7 fusion.4
  129.5 2.9 convolution_convert_fusion
  132.5 81.4 %all-gather.5.cloned.1.call-done = bf16[896,3584]{0,1:T(8,128)(2,1)} async-done(((bf16[896,448]{0,1:T(8,128)(2,1)}), bf16[896,3584]{0,1:T(8,128)(2,1)}) %all-gather.5.cloned.1.call-update) | async-done | bytes 6422544 | tf_op jit(solution)/shard_map/all_gather | solution.py:96
  213.9 4.9 %fusion.38 = f32[256,3584]{1,0:T(8,128)S(1)} fusion(bf16[256,896]{0,1:T(8,128)(2,1)S(1)} %bitcast.110, bf16[896,3584]{0,1:T(8,128)(2,1)} %all-gather.5.cloned.1.call-done), kind=kOutput, calls=%fused_computation.67 | convolution fusion | flops 1644167168 | bytes 10551296 | tf_op jit(solution)/shard_map/mtf,fe->mte/dot_general | solution.py:93
  218.9 3.7 fusion.2
  222.6 8.8 %copy.54 = bf16[1,256,3584]{1,0,2:T(2,128)(2,1)} copy(bf16[1,256,3584]{2,1,0:T(8,128)(2,1)} %fusion.2) | data formatting | bytes 3670016
  231.4 3.6 copy.62
  235.0 3.2 copy.46
  238.8 20.8 %reduce.4 = bf16[3584,4]{1,0:T(8,128)(2,1)S(1)} reduce(bf16[3584,1,4]{2,1,0:T(2,128)(2,1)} %bitcast.105, bf16[]{:T(256)} %broadcast.87), dimensions={1}, to_apply=%bitcast.83.reduce_sub_computation | reduce | bytes 57346
  259.6 2.2 reshape.258
  261.8 3.6 all-to-all-start.1
  265.4 3.2 copy.37
  268.6 20.7 %reduce.3 = bf16[3584,4]{1,0:T(8,128)(2,1)S(1)} reduce(bf16[3584,1,4]{2,1,0:T(2,128)(2,1)} %bitcast.106, bf16[]{:T(256)} %broadcast.87), dimensions={1}, to_apply=%bitcast.81.reduce_sub_computation | reduce | bytes 57346
  289.3 2.2 reshape.256
  292.2 5.7 %all-to-all-start = ((bf16[8,2,896]{2,1,0:T(2,128)(2,1)}), bf16[8,2,896]{2,1,0:T(2,128)(2,1)S(1)}, u32[]{:S(2)}, u32[]{:S(2)}) async-start(bf16[8,2,896]{2,1,0:T(2,128)(2,1)} %reshape.256), calls=%async_computation | async-start | bytes 57344 | tf_op jit(solution)/shard_map/all_to_all | solution.py:117
  297.8 31.3 %all_gather.19 = bf16[8,896,4]{1,2,0:T(4,128)(2,1)S(1)} all-gather(bf16[1,896,4]{1,2,0:T(4,128)(2,1)S(1)} %copy-done.8), channel_id=1, replica_groups=mesh['pop'=8,'mp'=4] {'pop'}, dimensions={0}, use_global_device_ids=true | all-gather | bytes 64512 | tf_op jit(solution)/shard_map/all_gather | solution.py:115
  329.1 30.7 %all_gather.18 = bf16[8,4,896]{2,1,0:T(4,128)(2,1)S(1)} all-gather(bf16[1,4,896]{2,1,0:T(4,128)(2,1)S(1)} %copy-done.9), channel_id=1, replica_groups=mesh['pop'=8,'mp'=4] {'pop'}, dimensions={0}, use_global_device_ids=true | all-gather | bytes 64512 | tf_op jit(solution)/shard_map/all_gather | solution.py:114
  359.8 3.3 reshape.259
  363.2 3.6 copy.47
  367.0 3.3 reshape.257
  370.3 4.6 bitcast_convert_fusion
  378.0 1.9 fusion.8
  379.8 6.3 %psum.21 = f32[1]{0:T(128)} all-reduce(f32[1]{0:T(128)} %bitcast.27), channel_id=1, replica_groups=mesh['pop'=8,'mp'=4] {'mp'}, use_global_device_ids=true, to_apply=%region_4.5 | all-reduce | flops 1 | bytes 8 | tf_op jit(solution)/shard_map/psum | solution.py:106
  387.2 21.8 %psum.22 = f32[]{:T(128)} all-reduce(f32[]{:T(128)} %bitcast.28), channel_id=1, replica_groups=mesh['pop'=8,'mp'=4] {'pop'}, use_global_device_ids=true, to_apply=%region_5.6 | all-reduce | flops 1 | bytes 8 | tf_op jit(solution)/shard_map/psum | solution.py:109
  412.1 18.3 %psum.23 = f32[]{:T(128)} all-reduce(f32[]{:T(128)} %bitcast.30), channel_id=1, replica_groups=mesh['pop'=8,'mp'=4] {'pop'}, use_global_device_ids=true, to_apply=%region_6.7 | all-reduce | flops 1 | bytes 8 | tf_op jit(solution)/shard_map/psum | solution.py:110
  431.1 1.9 divide_dynamic-update-slice_fusion
  433.0 2.1 copy.44
  435.2 19.1 %all-reduce = f32[8]{0:T(128)S(1)} all-reduce(f32[8]{0:T(128)S(1)} %divide_dynamic-update-slice_fusion), channel_id=1, replica_groups=mesh['pop'=8,'mp'=4] {'pop'}, use_global_device_ids=true, to_apply=%add | all-reduce | flops 8 | bytes 64
  454.4 2.0 convolution_multiply_fusion.1
  456.4 2.1 bitcast_multiply_fusion
  (55 shorter events, 17.5 us)
Async XLA Ops:
  7.2 2.8 copy-start
  7.2 2.8 copy-start.2
  7.2 106.0 %all-gather.3.cloned.1.call-start = ((), (), s32[]{:S(2)}) async-start(), calls=%async_computation.3 | async-start | bytes 7225344 | tf_op jit(solution)/shard_map/all_gather | solution.py:57
  7.9 206.0 %all-gather.5.cloned.1.call-start = ((), (), s32[]{:S(2)}) async-start(), calls=%async_computation.4 | async-start | bytes 7225344 | tf_op jit(solution)/shard_map/all_gather | solution.py:96
  8.7 366.2 %reduce-scatter.4.cloned.1.call-start = ((), (), s32[]{:S(2)}) async-start(), calls=%async_computation.5 | async-start | bytes 2293760
  12.2 105.9 %copy-start.6 = (bf16[1,3584,4]{1,2,0:T(4,128)(2,1)S(1)}, bf16[1,3584,4]{1,2,0:T(4,128)(2,1)}, u32[]{:S(2)}) copy-start(bf16[1,3584,4]{1,2,0:T(4,128)(2,1)} %param.17) | copy-start | bytes 86020
  12.2 105.9 %copy-start.9 = (bf16[1,4,896]{2,1,0:T(4,128)(2,1)S(1)}, bf16[1,4,896]{2,1,0:T(4,128)(2,1)}, u32[]{:S(2)}) copy-start(bf16[1,4,896]{2,1,0:T(4,128)(2,1)} %param.18) | copy-start | bytes 21508
  125.9 1.4 copy-start.3
  125.9 1.4 copy-start.4
  127.9 1.2 copy-start.1
  129.4 2.9 copy-start.8
  132.5 86.4 %copy-start.5 = (bf16[1,4,3584]{2,1,0:T(4,128)(2,1)S(1)}, bf16[1,4,3584]{2,1,0:T(4,128)(2,1)}, u32[]{:S(2)}) copy-start(bf16[1,4,3584]{2,1,0:T(4,128)(2,1)} %param.20) | copy-start | bytes 86020
  238.8 26.6 %copy-start.7 = (bf16[1,3584,4]{1,2,0:T(4,128)(2,1)S(1)}, bf16[1,3584,4]{1,2,0:T(4,128)(2,1)}, u32[]{:S(2)}) copy-start(bf16[1,3584,4]{1,2,0:T(4,128)(2,1)} %param.17) | copy-start | bytes 86020
  261.8 30.4 %all-to-all-start.1 = ((bf16[8,2,896]{2,1,0:T(2,128)(2,1)}), bf16[8,2,896]{2,1,0:T(2,128)(2,1)S(1)}, u32[]{:S(2)}, u32[]{:S(2)}) async-start(bf16[8,2,896]{2,1,0:T(2,128)(2,1)} %reshape.258), calls=%async_computation.1 | async-start | bytes 57344 | tf_op jit(solution)/shard_map/all_to_all | solution.py:118
  268.6 23.0 %copy-start.10 = (u32[32]{0:T(128)S(1)}, u32[32]{0:T(128)}, u32[]{:S(2)}) copy-start(u32[32]{0:T(128)} %constant.59) | copy-start | bytes 388
  292.2 74.8 %all-to-all-start = ((bf16[8,2,896]{2,1,0:T(2,128)(2,1)}), bf16[8,2,896]{2,1,0:T(2,128)(2,1)S(1)}, u32[]{:S(2)}, u32[]{:S(2)}) async-start(bf16[8,2,896]{2,1,0:T(2,128)(2,1)} %reshape.256), calls=%async_computation | async-start | bytes 57344 | tf_op jit(solution)/shard_map/all_to_all | solution.py:117
Sparse Core Ops, SparseCore 0:
  10.2 103.0 all-gather.2
  115.4 98.4 all-gather.4
  235.2 27.7 reduce-scatter.3
where the time goes:
time: 466 us; the launch traced here: 465 us
  waiting for transfers between devices  184 us (39%)
  blocking collectives  127 us (27%)
  other arithmetic  53.7 us (12%)
  local copies, waits for them, and re-layouts  46.4 us (10%)
  matrix products  24.7 us (5%)
  between operations  19.6 us (4%)
  starting transfers between devices  9.34 us (2%)
    all_gather x1, waiting for transfers between devices, per_device(): lax.all_gather(w_query, 'pop', axis=0, tiled=True)  101 us
    all_gather x1, waiting for transfers between devices, per_device(): lax.all_gather(w_out, 'pop', axis=1, tiled=True)  81.4 us
    unnamed x3, other arithmetic  43.4 us
    unnamed x37, local copies, waits for them, and re-layouts  38 us
    all_gather x1, blocking collectives, per_device(): lax.all_gather(o_left, 'pop', axis=0, tiled=True)  31.3 us
    all_gather x1, blocking collectives, per_device(): lax.all_gather(query_right_factors, 'pop', axis=0, tiled=True)  30.7 us
    psum x1, blocking collectives, per_device(): mean = lax.psum(jnp.sum(fitness), 'pop') / count  21.8 us
    unnamed x1, blocking collectives  19.1 us
  transfers between devices with their start and end apart: 5, of which 2 were waited for; matrix products, arithmetic and copies ran while one was open for 19% of the time, Pallas kernels for 0%

commit v1 on v0

--- a/solution.py
+++ b/solution.py
@@ -112,7 +112,9 @@
     every_weight = lax.all_gather(weight, "pop", axis=0, tiled=True)
     right_factors_gathered, left_all = (
         lax.all_gather(query_right_factors, "pop", axis=0, tiled=True),
-        lax.all_gather(o_left, "pop", axis=0, tiled=True),
+        jnp.concatenate(
+            lax.all_to_all(jnp.stack([o_left] * lax.axis_size("pop")), "pop", 0, 0), axis=0
+        ),
     )
     rows_q = lax.all_to_all(query_left_factors, "pop", split_axis=1, concat_axis=0, tiled=True)
     cols_o = lax.all_to_all(o_right, "pop", split_axis=2, concat_axis=0, tiled=True)

time: 466 us -> 443 us (0.951)
  blocking collectives: 127 us -> 97.4 us
  starting transfers between devices: 9.34 us -> 14.7 us
    all_gather x1 -> x0, blocking collectives: 31.3 us -> none  [per_device(): lax.all_gather(o_left, 'pop', axis=0, tiled=True)]
    all_to_all x0 -> x1, starting transfers between devices: none -> 5.39 us  [per_device(): lax.all_to_all(jnp.stack([o_left] * lax.axis_size('pop')), 'pop', 0, 0)]
    unnamed x37 -> x39, local copies, waits for them, and re-layouts: 38 us -> 38.3 us
  transfers between devices with their start and end apart: 5 -> 6, of which waited for: 2 -> 2; matrix products, arithmetic and copies ran while one was open for 19% -> 22% of each run, Pallas kernels for 0% -> 0%
where the time goes in v1:
time: 443 us; the launch traced here: 441 us
  waiting for transfers between devices  184 us (42%)
  blocking collectives  97.4 us (22%)
  other arithmetic  53.8 us (12%)
  local copies, waits for them, and re-layouts  47.3 us (11%)
  matrix products  24.4 us (6%)
  between operations  19.7 us (4%)
  starting transfers between devices  14.7 us (3%)
    all_gather x1, waiting for transfers between devices, per_device(): lax.all_gather(w_query, 'pop', axis=0, tiled=True)  101 us
    all_gather x1, waiting for transfers between devices, per_device(): lax.all_gather(w_out, 'pop', axis=1, tiled=True)  81.4 us
    unnamed x3, other arithmetic  43.5 us
    unnamed x39, local copies, waits for them, and re-layouts  38.3 us
    all_gather x1, blocking collectives, per_device(): lax.all_gather(query_right_factors, 'pop', axis=0, tiled=True)  31.3 us
    psum x1, blocking collectives, per_device(): mean = lax.psum(jnp.sum(fitness), 'pop') / count  22.4 us
    unnamed x1, blocking collectives  19.1 us
    psum x1, blocking collectives, per_device(): lax.psum(jnp.sum((fitness - mean) * (fitness - mean)), 'pop') / count  18.3 us
  transfers between devices with their start and end apart: 6, of which 2 were waited for; matrix products, arithmetic and copies ran while one was open for 22% of the time, Pallas kernels for 0%

profile of v1, /device:TPU:0, one launch (start us, length us, event | category | flops | bytes accessed | tf_op | source)
XLA Modules:
  0.0 441.1 jit_solution(6073753491619328331)
XLA Ops:
  12.2 101.0 %all-gather.3.cloned.1.call-done = bf16[3584,896]{1,0:T(8,128)(2,1)} async-done(((bf16[448,896]{1,0:T(8,128)(2,1)}), bf16[3584,896]{1,0:T(8,128)(2,1)}) %all-gather.3.cloned.1.call-update) | async-done | bytes 6422544 | tf_op jit(solution)/shard_map/all_gather | solution.py:57
  113.2 4.9 %fusion.38 = f32[256,896]{1,0:T(8,128)S(1)} fusion(bf16[256,3584]{1,0:T(8,128)(2,1)S(1)} %copy-done, bf16[3584,896]{1,0:T(8,128)(2,1)} %all-gather.3.cloned.1.call-done), kind=kOutput, calls=%fused_computation.67 | convolution fusion | flops 1644167168 | bytes 9175040 | tf_op jit(solution)/shard_map/dot_general | solution.py:55
  118.1 2.7 fusion.4
  129.8 2.6 convolution_convert_fusion
  132.6 81.4 %all-gather.5.cloned.1.call-done = bf16[896,3584]{0,1:T(8,128)(2,1)} async-done(((bf16[896,448]{0,1:T(8,128)(2,1)}), bf16[896,3584]{0,1:T(8,128)(2,1)}) %all-gather.5.cloned.1.call-update) | async-done | bytes 6422544 | tf_op jit(solution)/shard_map/all_gather | solution.py:96
  213.9 4.9 %fusion.39 = f32[256,3584]{1,0:T(8,128)S(1)} fusion(bf16[256,896]{0,1:T(8,128)(2,1)S(1)} %bitcast.113, bf16[896,3584]{0,1:T(8,128)(2,1)} %all-gather.5.cloned.1.call-done), kind=kOutput, calls=%fused_computation.68 | convolution fusion | flops 1644167168 | bytes 10551296 | tf_op jit(solution)/shard_map/mtf,fe->mte/dot_general | solution.py:93
  218.9 3.7 fusion.2
  222.6 8.8 %copy.55 = bf16[1,256,3584]{1,0,2:T(2,128)(2,1)} copy(bf16[1,256,3584]{2,1,0:T(8,128)(2,1)} %fusion.2) | data formatting | bytes 3670016
  231.4 3.6 copy.63
  235.0 3.2 copy.47
  238.8 20.8 %reduce.4 = bf16[3584,4]{1,0:T(8,128)(2,1)S(1)} reduce(bf16[3584,1,4]{2,1,0:T(2,128)(2,1)} %bitcast.108, bf16[]{:T(256)} %broadcast.90), dimensions={1}, to_apply=%bitcast.86.reduce_sub_computation | reduce | bytes 57346
  259.6 2.2 reshape.265
  261.8 3.6 all-to-all-start.2
  265.4 3.2 copy.38
  268.6 20.7 %reduce.3 = bf16[3584,4]{1,0:T(8,128)(2,1)S(1)} reduce(bf16[3584,1,4]{2,1,0:T(2,128)(2,1)} %bitcast.109, bf16[]{:T(256)} %broadcast.90), dimensions={1}, to_apply=%bitcast.84.reduce_sub_computation | reduce | bytes 57346
  289.3 2.2 reshape.263
  291.5 5.7 %all-to-all-start = ((bf16[8,2,896]{2,1,0:T(2,128)(2,1)}), bf16[8,2,896]{2,1,0:T(2,128)(2,1)S(1)}, u32[]{:S(2)}, u32[]{:S(2)}) async-start(bf16[8,2,896]{2,1,0:T(2,128)(2,1)} %reshape.263), calls=%async_computation | async-start | bytes 57344 | tf_op jit(solution)/shard_map/all_to_all | solution.py:119
  297.8 31.3 %all_gather.15 = bf16[8,4,896]{2,1,0:T(4,128)(2,1)S(1)} all-gather(bf16[1,4,896]{2,1,0:T(4,128)(2,1)S(1)} %copy-done.8), channel_id=1, replica_groups=mesh['pop'=8,'mp'=4] {'pop'}, dimensions={0}, use_global_device_ids=true | all-gather | bytes 64512 | tf_op jit(solution)/shard_map/all_gather | solution.py:114
  329.1 3.3 reshape.266
  332.4 3.6 copy.48
  336.8 5.4 %all-to-all-start.1 = ((bf16[8,1,896,4]{2,3,1,0:T(4,128)(2,1)}), bf16[8,1,896,4]{2,3,1,0:T(4,128)(2,1)S(1)}, u32[]{:S(2)}, u32[]{:S(2)}) async-start(bf16[8,1,896,4]{2,3,1,0:T(4,128)(2,1)} %stack.2), calls=%async_computation.1 | async-start | bytes 114688 | tf_op jit(solution)/shard_map/all_to_all | solution.py:116
  342.2 3.3 reshape.264
  345.5 4.6 %bitcast_convert_fusion = f32[1,3584,4]{2,0,1:T(1,128)} fusion(bf16[3584,1,4]{2,1,0:T(2,128)(2,1)} %reshape.264), kind=kLoop, calls=%fused_computation.66 | loop fusion | flops 14336 | bytes 86016 | tf_op jit(solution)/shard_map/convert_element_type | solution.py:123
  353.2 1.9 fusion.8
  355.1 6.3 %psum.21 = f32[1]{0:T(128)} all-reduce(f32[1]{0:T(128)} %bitcast.27), channel_id=1, replica_groups=mesh['pop'=8,'mp'=4] {'mp'}, use_global_device_ids=true, to_apply=%region_4.5 | all-reduce | flops 1 | bytes 8 | tf_op jit(solution)/shard_map/psum | solution.py:106
  362.6 22.4 %psum.22 = f32[]{:T(128)} all-reduce(f32[]{:T(128)} %bitcast.28), channel_id=1, replica_groups=mesh['pop'=8,'mp'=4] {'pop'}, use_global_device_ids=true, to_apply=%region_5.6 | all-reduce | flops 1 | bytes 8 | tf_op jit(solution)/shard_map/psum | solution.py:109
  388.2 18.3 %psum.23 = f32[]{:T(128)} all-reduce(f32[]{:T(128)} %bitcast.30), channel_id=1, replica_groups=mesh['pop'=8,'mp'=4] {'pop'}, use_global_device_ids=true, to_apply=%region_6.7 | all-reduce | flops 1 | bytes 8 | tf_op jit(solution)/shard_map/psum | solution.py:110
  407.1 2.0 divide_dynamic-update-slice_fusion
  409.2 2.1 copy.45
  411.3 19.1 %all-reduce = f32[8]{0:T(128)S(1)} all-reduce(f32[8]{0:T(128)S(1)} %divide_dynamic-update-slice_fusion), channel_id=1, replica_groups=mesh['pop'=8,'mp'=4] {'pop'}, use_global_device_ids=true, to_apply=%add | all-reduce | flops 8 | bytes 64
  430.6 2.0 convolution_multiply_fusion.1
  432.6 2.1 bitcast_multiply_fusion
  (59 shorter events, 18.4 us)
Async XLA Ops:
  7.2 2.8 copy-start
  7.2 2.8 copy-start.2
  7.2 106.0 %all-gather.3.cloned.1.call-start = ((), (), s32[]{:S(2)}) async-start(), calls=%async_computation.4 | async-start | bytes 7225344 | tf_op jit(solution)/shard_map/all_gather | solution.py:57
  7.9 206.0 %all-gather.5.cloned.1.call-start = ((), (), s32[]{:S(2)}) async-start(), calls=%async_computation.5 | async-start | bytes 7225344 | tf_op jit(solution)/shard_map/all_gather | solution.py:96
  8.7 341.4 %reduce-scatter.4.cloned.1.call-start = ((), (), s32[]{:S(2)}) async-start(), calls=%async_computation.6 | async-start | bytes 2293760
  12.2 106.0 %copy-start.6 = (bf16[1,3584,4]{1,2,0:T(4,128)(2,1)S(1)}, bf16[1,3584,4]{1,2,0:T(4,128)(2,1)}, u32[]{:S(2)}) copy-start(bf16[1,3584,4]{1,2,0:T(4,128)(2,1)} %param.17) | copy-start | bytes 86020
  12.2 106.0 %copy-start.8 = (bf16[1,4,896]{2,1,0:T(4,128)(2,1)S(1)}, bf16[1,4,896]{2,1,0:T(4,128)(2,1)}, u32[]{:S(2)}) copy-start(bf16[1,4,896]{2,1,0:T(4,128)(2,1)} %param.18) | copy-start | bytes 21508
  125.9 1.4 copy-start.3
  125.9 1.4 copy-start.4
  127.9 1.3 copy-start.1
  127.9 1.8 copy-start.10
  129.8 2.6 copy-start.9
  132.5 86.3 %copy-start.5 = (bf16[1,4,3584]{2,1,0:T(4,128)(2,1)S(1)}, bf16[1,4,3584]{2,1,0:T(4,128)(2,1)}, u32[]{:S(2)}) copy-start(bf16[1,4,3584]{2,1,0:T(4,128)(2,1)} %param.20) | copy-start | bytes 86020
  238.8 26.6 %copy-start.7 = (bf16[1,3584,4]{1,2,0:T(4,128)(2,1)S(1)}, bf16[1,3584,4]{1,2,0:T(4,128)(2,1)}, u32[]{:S(2)}) copy-start(bf16[1,3584,4]{1,2,0:T(4,128)(2,1)} %param.17) | copy-start | bytes 86020
  261.8 29.8 %all-to-all-start.2 = ((bf16[8,2,896]{2,1,0:T(2,128)(2,1)}), bf16[8,2,896]{2,1,0:T(2,128)(2,1)S(1)}, u32[]{:S(2)}, u32[]{:S(2)}) async-start(bf16[8,2,896]{2,1,0:T(2,128)(2,1)} %reshape.265), calls=%async_computation.2 | async-start | bytes 57344 | tf_op jit(solution)/shard_map/all_to_all | solution.py:120
  268.6 28.6 %copy-start.11 = (u32[32]{0:T(128)S(1)}, u32[32]{0:T(128)}, u32[]{:S(2)}) copy-start(u32[32]{0:T(128)} %constant.59) | copy-start | bytes 388
  291.5 44.6 %all-to-all-start = ((bf16[8,2,896]{2,1,0:T(2,128)(2,1)}), bf16[8,2,896]{2,1,0:T(2,128)(2,1)S(1)}, u32[]{:S(2)}, u32[]{:S(2)}) async-start(bf16[8,2,896]{2,1,0:T(2,128)(2,1)} %reshape.263), calls=%async_computation | async-start | bytes 57344 | tf_op jit(solution)/shard_map/all_to_all | solution.py:119
  336.8 93.6 %all-to-all-start.1 = ((bf16[8,1,896,4]{2,3,1,0:T(4,128)(2,1)}), bf16[8,1,896,4]{2,3,1,0:T(4,128)(2,1)S(1)}, u32[]{:S(2)}, u32[]{:S(2)}) async-start(bf16[8,1,896,4]{2,3,1,0:T(4,128)(2,1)} %stack.2), calls=%async_computation.1 | async-start | bytes 114688 | tf_op jit(solution)/shard_map/all_to_all | solution.py:116
Sparse Core Ops, SparseCore 0:
  10.2 103.0 all-gather.2
  115.4 98.4 all-gather.4
  235.2 27.7 reduce-scatter.3
